TPU v7x, 32 devices: a whole 2x2x4 slice. The times are simulated.
32 devices in a mesh: sub: 8 (over z, y), inner: 4 (over x, core).
Axes of the slice: x: 2, y: 2, z: 4, core: 2. Of those that a mesh axis runs over, the one named last changes fastest.
Arguments:
- solution: float32 [32, 3, 32, 16, 128], P(None, None, 'sub', 'inner'), may hold values from -6 to 6
- residual: float32 [32, 3, 32, 16, 128], P(None, None, 'sub', 'inner'), may hold values from -6 to 6
- direction: float32 [32, 3, 32, 16, 128], P(None, None, 'sub', 'inner'), may hold values from -6 to 6
- mass: float32 [32, 16, 128], P('sub', 'inner'), may hold values from 0.2 to 5
- coarse_basis: float32 [32, 3, 32, 16, 128], P(None, None, 'sub', 'inner'), may hold values from -1 to 1
- line_inverse: float32 [8, 4, 128, 128], P('sub', 'inner'), may hold values from -1.5 to 1.5
- coarse_factor: float32 [1024, 1024], P(('sub', 'inner')), may hold values from -1 to 1
Outputs:
- new_solution: float32 [32, 3, 32, 16, 128], P(None, None, 'sub', 'inner')
- new_residual: float32 [32, 3, 32, 16, 128], P(None, None, 'sub', 'inner')
- new_direction: float32 [32, 3, 32, 16, 128], P(None, None, 'sub', 'inner')
All inputs are finite; a program needn't handle non-finite values.
Results may differ from a plain program's by a relative error of at most 0.00017.
Values sent between devices are 32-bit elements; how exact they have to be, the bound alone decides.
A program may use at most 64 MiB of HBM per device.

v0:
```python
import jax
import jax.numpy as jnp
from jax import lax
from jax.sharding import PartitionSpec as P

exact_mode = lax.Precision.HIGHEST


def with_halo(array, sides, width):
    for axis, dim in sides:
        count, length = (lax.axis_size(axis), array.shape[dim])
        up = [(i, (i + 1) % count) for i in range(count - 1)]
        down = [(j, i) for i, j in up]
        last = lax.slice_in_dim(array, length - width, length, axis=dim)
        initial = lax.slice_in_dim(array, 0, width, axis=dim)
        before = lax.ppermute(last, axis, up)
        after = lax.ppermute(initial, axis, down)
        array = jnp.concatenate([before, array, after], axis=dim)
    return array


def shifted(padded, which, offset):
    window = [slice(None), slice(None)]
    for place in (2, 3, 4):
        length = padded.shape[place]
        if place == which:
            window.append(slice(2 + offset, length - 2 + offset))
        else:
            window.append(slice(2, length - 2))
    return padded[tuple(window)]


def operate(direction, mass):
    widened = with_halo(direction, (("sub", 2), ("inner", 3)), 2)
    padded = jnp.pad(widened, ((0, 0), (0, 0), (0, 0), (0, 0), (2, 2)))
    center = shifted(padded, 2, 0)
    nearby = jnp.zeros_like(center)
    farther = jnp.zeros_like(center)
    for which in (2, 3, 4):
        nearby = nearby + shifted(padded, which, 1) + shifted(padded, which, -1)
        farther = farther + shifted(padded, which, 2) + shifted(padded, which, -2)
    return (mass + 7.5) * center - 4.0 / 3.0 * nearby + 1.0 / 12.0 * farther


def spd_solve(lower, rhs):
    middle = lax.linalg.triangular_solve(lower, rhs, left_side=True, lower=True)
    return lax.linalg.triangular_solve(lower, middle, left_side=True, lower=True, transpose_a=True)


def along_lines(flat, inverse):
    lines = flat.reshape(-1, inverse.shape[0])
    return jnp.dot(lines, inverse.T, precision=exact_mode).reshape(flat.shape)


def product(left, right):
    return jnp.dot(left, right.T, precision=exact_mode)


def on_device(solution, residual, direction, mass, coarse_basis, line_inverse, coarse_factor):
    directions = direction.shape[0]
    shape = direction.shape
    inverse = line_inverse[0, 0]
    image = operate(direction, mass)
    flat_p = direction.reshape(directions, -1)
    flat_q = image.reshape(directions, -1)
    flat_r = residual.reshape(directions, -1)
    flat_s = solution.reshape(directions, -1)
    basis_flat = coarse_basis.reshape(coarse_basis.shape[0], -1)
    lined_r = along_lines(flat_r, inverse)
    lined_q = along_lines(flat_q, inverse)
    rhs_r = product(basis_flat, flat_r)
    rhs_q = product(basis_flat, flat_q)
    summed = lax.psum(
        (
            product(flat_p, flat_q),
            product(flat_p, flat_r),
            product(flat_q, lined_r),
            product(flat_q, lined_q),
            jnp.dot(coarse_factor.T, rhs_r, precision=exact_mode),
            jnp.dot(coarse_factor.T, rhs_q, precision=exact_mode),
        ),
        ("sub", "inner"),
    )
    gram_pq, proj_pr, image_lined_r, image_lined_q, mid_r, mid_q = summed
    lower = jnp.linalg.cholesky(gram_pq)
    alpha_mix = spd_solve(lower, proj_pr)
    flat_new = flat_r - jnp.dot(alpha_mix.T, flat_q, precision=exact_mode)
    local_part = lined_r - jnp.dot(alpha_mix.T, lined_q, precision=exact_mode)
    coarse_mid = mid_r - jnp.dot(mid_q, alpha_mix, precision=exact_mode)
    coarse_sol = jnp.dot(coarse_factor, coarse_mid, precision=exact_mode)
    precond = local_part + jnp.dot(coarse_sol.T, basis_flat, precision=exact_mode)
    cross_qz = (
        image_lined_r
        - jnp.dot(image_lined_q, alpha_mix, precision=exact_mode)
        + jnp.dot(mid_q.T, coarse_mid, precision=exact_mode)
    )
    new_solution = flat_s + jnp.dot(alpha_mix.T, flat_p, precision=exact_mode)
    beta_mix = -spd_solve(lower, cross_qz)
    new_direction = precond + jnp.dot(beta_mix.T, flat_p, precision=exact_mode)
    return (new_solution.reshape(shape), flat_new.reshape(shape), new_direction.reshape(shape))


def solution(mesh):
    placed = (
        P(None, None, "sub", "inner", None),
        P(None, None, "sub", "inner", None),
        P(None, None, "sub", "inner", None),
        P("sub", "inner", None),
        P(None, None, "sub", "inner", None),
        P("sub", "inner", None, None),
        P(("sub", "inner"), None),
    )
    return jax.shard_map(
        on_device,
        mesh=mesh,
        in_specs=placed,
        out_specs=(
            P(None, None, "sub", "inner", None),
            P(None, None, "sub", "inner", None),
            P(None, None, "sub", "inner", None),
        ),
        check_vma=False,
    )
```

profile of v0, /device:TPU:0, one launch (start us, length us, event | category | flops | bytes accessed | tf_op | source)
XLA Modules:
  0.0 269.1 jit_solution(2169634670247983347)
XLA Ops:
  7.2 1.3 fusion.37
  8.6 1.3 collective-permute-start
  10.7 6.4 %collective-permute-start.1 = (f32[32,3,2,4,128]{4,0,3,2,1:T(8,128)}, f32[32,3,2,4,128]{4,0,3,2,1:T(8,128)}, u32[]{:S(2)}, u32[]{:S(2)}) collective-permute-start(f32[32,3,2,4,128]{4,0,3,2,1:T(8,128)} %copy.83), channel_id=1, source_target_pairs={{0,4},{4,8},{8,12},{12,16},{16,20},{20,24},{24,28},{1,5},{5,9},{9,... | collective-permute-start | bytes 1179656 | tf_op jit(solution)/shard_map/ppermute | solution.py:16
  17.1 1.3 copy.42
  18.5 2.4 reshape.56
  20.9 1.2 reshape.58
  22.9 8.4 %collective-permute-done.1 = f32[32,3,2,4,128]{4,0,3,2,1:T(8,128)} collective-permute-done((f32[32,3,2,4,128]{4,0,3,2,1:T(8,128)}, f32[32,3,2,4,128]{4,0,3,2,1:T(8,128)}, u32[]{:S(2)}, u32[]{:S(2)}) %collective-permute-start.1) | collective-permute-done | bytes 393248 | tf_op jit(solution)/shard_map/ppermute | solution.py:16
  31.3 1.3 copy.47
  33.4 1.3 fusion.36
  34.6 1.3 collective-permute-start.2
  35.9 3.9 %collective-permute-start.3 = (f32[32,3,8,2,128]{4,2,3,1,0:T(8,128)}, f32[32,3,8,2,128]{4,2,3,1,0:T(8,128)}, u32[]{:S(2)}, u32[]{:S(2)}) collective-permute-start(f32[32,3,8,2,128]{4,2,3,1,0:T(8,128)} %get-tuple-element.11), channel_id=1, source_target_pairs={{0,1},{1,2},{2,3},{4,5},{5,6},{6,7},{8,9},{9,10},{10,11},{12,13},{... | collective-permute-start | bytes 2359304 | tf_op jit(solution)/shard_map/ppermute | solution.py:16
  39.8 1.7 fusion.23
  41.5 2.1 reshape.61
  43.7 1.2 reshape.63
  44.9 2.4 reshape.55
  50.6 6.0 %select_maximum_fusion = f32[32,3,8,8,132]{4,2,3,1,0:T(8,128)S(1)} fusion(f32[32,3,8,2,128]{4,2,3,1,0:T(8,128)} %collective-permute-done.2, f32[32,3,8,2,128]{4,2,3,1,0:T(8,128)} %collective-permute-done.3, f32[32,3,2,4,128]{4,2,3,1,0:T(2,128)} %copy-done.5, f32[32,3,4,4,128]{4,2,3,1,0:T(4,128)S(1)} %copy.42, f32[32,3,2,4,128]{4,2,3,1,0:T(2,128)} %copy-done.7), kind=kLoop, calls=%fused_computation.7 | loop fusion | flops 9732096 | bytes 6389760 | tf_op jit(solution)/shard_map/concatenate | solution.py:18
  56.7 5.1 %fusion.9 = f32[32,3,4,4,128]{4,2,3,1,0:T(4,128)S(1)} fusion(f32[32,3,2,4,128]{4,2,3,1,0:T(2,128)S(1)} %copy-done.8, f32[32,3,4,4,128]{4,2,3,1,0:T(4,128)S(1)} %copy.42, f32[32,3,2,4,128]{4,2,3,1,0:T(2,128)S(1)} %copy-done.6, f32[32,3,8,8,132]{4,2,3,1,0:T(8,128)S(1)} %select_maximum_fusion, f32[32,3,8,2,128]{4,2,3,1,0:T(8,128)} %collective-permute-done.3, ...), kind=kLoop, calls=%fused_computation.35 | loop fusion | flops 6094848 | bytes 7086080 | tf_op jit(solution)/shard_map/add | solution.py:42
  63.2 1.2 convolution_bitcast_fusion.2
  66.4 1.9 fusion.39
  68.3 42.4 %all-reduce.1 = (f32[32,32]{1,0:T(8,128)S(1)}, f32[32,32]{0,1:T(8,128)S(1)}, f32[32,32]{1,0:T(8,128)S(1)}, f32[32,32]{1,0:T(8,128)S(1)}) all-reduce(f32[32,32]{1,0:T(8,128)S(1)} %convolution_bitcast_fusion.4, f32[32,32]{0,1:T(8,128)S(1)} %convolution_bitcast_fusion.5, ...), channel_id=1, replica_groups=mesh['sub'=8,'inner'=4] {'sub','inner'}, use_global_device_ids=true, to_apply=%region_3.4 | all-reduce | flops 4096 | bytes 32768 | tf_op jit(solution)/shard_map/psum | solution.py:73
  110.8 2.9 %cholesky.18 = f32[32,32]{1,0:T(8,128)S(1)} custom-call(f32[32,32]{1,0:T(8,128)S(1)} %fusion.33), custom_call_target="Cholesky" | custom-call | tf_op jit(solution)/shard_map/jit(cholesky)/cholesky | solution.py:85
  115.0 2.4 custom-call.12
  118.8 2.8 %convolution_subtract_fusion = f32[32,6144]{1,0:T(8,128)} fusion(f32[32,6144]{1,0:T(8,128)} %reshape.61, f32[32,32]{1,0:T(8,128)S(1)} %fusion.31, f32[32,6144]{1,0:T(8,128)S(1)} %reshape.62), kind=kOutput, calls=%fused_computation.4 | convolution fusion | flops 75694080 | bytes 2363392 | tf_op jit(solution)/shard_map/dot_general | solution.py:88
  121.6 2.0 convolution_subtract_fusion.1
  123.6 1.4 reshape.60
  125.0 1.9 convolution_add_fusion.2
  126.9 1.4 reshape.57
  128.5 126.6 %all-reduce.5.cloned.1.call-done = (f32[1024,32]{0,1:T(8,128)}, f32[1024,32]{0,1:T(8,128)}) async-done(((f32[1024,32]{0,1:T(8,128)}, f32[1024,32]{0,1:T(8,128)}), (f32[1024,32]{0,1:T(8,128)}, f32[1024,32]{0,1:T(8,128)})) %all-reduce.5.cloned.1.call-update) | async-done | bytes 262160 | tf_op jit(solution)/shard_map/psum | solution.py:73
  255.1 1.3 convolution_subtract_fusion.2
  256.6 1.2 convolution_add_fusion.3
  258.1 1.9 convolution_add_fusion.1
  260.9 1.4 reshape.64
  (57 shorter events, 13.5 us)
Async XLA Ops:
  7.2 42.4 %copy-start = (f32[32,1024]{1,0:T(8,128)S(1)}, f32[32,1024]{1,0:T(8,128)}, u32[]{:S(2)}) copy-start(f32[32,1024]{1,0:T(8,128)} %param.17) | copy-start | bytes 393220
  7.2 13.7 %copy-start.11 = (f32[4,4,128]{2,1,0:T(4,128)S(1)}, f32[4,4,128]{2,1,0:T(4,128)}, u32[]{:S(2)}) copy-start(f32[4,4,128]{2,1,0:T(4,128)} %param.14) | copy-start | bytes 24580
  7.2 13.7 %copy-start.2 = (f32[32,3,4,4,128]{4,3,2,1,0:T(4,128)S(1)}, f32[32,3,4,4,128]{4,3,2,1,0:T(4,128)}, u32[]{:S(2)}) copy-start(f32[32,3,4,4,128]{4,3,2,1,0:T(4,128)} %param.12) | copy-start | bytes 2359300
  7.2 247.9 %all-reduce.5.cloned.1.call-start = ((), (), s32[]{:S(2)}) async-start(), calls=%async_computation | async-start | bytes 524288 | tf_op jit(solution)/shard_map/psum | solution.py:73
  8.6 14.0 %collective-permute-start = (f32[32,3,2,4,128]{4,0,3,2,1:T(8,128)S(1)}, f32[32,3,2,4,128]{4,0,3,2,1:T(8,128)S(1)}, u32[]{:S(2)}, u32[]{:S(2)}) collective-permute-start(f32[32,3,2,4,128]{4,0,3,2,1:T(8,128)S(1)} %copy.84), channel_id=1, source_target_pairs={{4,0},{8,4},{12,8},{16,12},{20,16},{24,20},{28,24},{5,1},{9,5},{13... | collective-permute-start | bytes 1179656 | tf_op jit(solution)/shard_map/ppermute | solution.py:17
  10.7 29.1 %copy-start.10 = (f32[1,1,128,128]{3,2,1,0:T(8,128)S(1)}, f32[1,1,128,128]{3,2,1,0:T(8,128)}, u32[]{:S(2)}) copy-start(f32[1,1,128,128]{3,2,1,0:T(8,128)} %param.16) | copy-start | bytes 196612
  10.7 20.6 %collective-permute-start.1 = (f32[32,3,2,4,128]{4,0,3,2,1:T(8,128)}, f32[32,3,2,4,128]{4,0,3,2,1:T(8,128)}, u32[]{:S(2)}, u32[]{:S(2)}) collective-permute-start(f32[32,3,2,4,128]{4,0,3,2,1:T(8,128)} %copy.83), channel_id=1, source_target_pairs={{0,4},{4,8},{8,12},{12,16},{16,20},{20,24},{24,28},{1,5},{5,9},{9,... | collective-permute-start | bytes 1179656 | tf_op jit(solution)/shard_map/ppermute | solution.py:16
  20.9 22.8 %copy-start.3 = (f32[32,3,4,4,128]{4,3,2,1,0:T(4,128)S(1)}, f32[32,3,4,4,128]{4,3,2,1,0:T(4,128)}, u32[]{:S(2)}) copy-start(f32[32,3,4,4,128]{4,3,2,1,0:T(4,128)} %param.15) | copy-start | bytes 2359300
  22.9 9.7 %copy-start.5 = (f32[32,3,2,4,128]{4,2,3,1,0:T(2,128)}, f32[32,3,2,4,128]{4,2,3,1,0:T(2,128)S(1)}, u32[]{:S(2)}) copy-start(f32[32,3,2,4,128]{4,2,3,1,0:T(2,128)S(1)} %copy.45) | copy-start | bytes 1179652
  32.6 0.8 copy-start.7
  32.6 14.6 %copy-start.1 = (f32[32,3,4,4,128]{4,3,2,1,0:T(4,128)S(1)}, f32[32,3,4,4,128]{4,3,2,1,0:T(4,128)}, u32[]{:S(2)}) copy-start(f32[32,3,4,4,128]{4,3,2,1,0:T(4,128)} %param.13) | copy-start | bytes 2359300
  34.6 16.0 %collective-permute-start.2 = (f32[32,3,8,2,128]{4,2,3,1,0:T(8,128)}, f32[32,3,8,2,128]{4,2,3,1,0:T(8,128)}, u32[]{:S(2)}, u32[]{:S(2)}) collective-permute-start(f32[32,3,8,2,128]{4,2,3,1,0:T(8,128)} %get-tuple-element.12), channel_id=1, source_target_pairs={{1,0},{2,1},{3,2},{5,4},{6,5},{7,6},{9,8},{10,9},{11,10},{13,12},{... | collective-permute-start | bytes 2359304 | tf_op jit(solution)/shard_map/ppermute | solution.py:17
  35.9 14.7 %collective-permute-start.3 = (f32[32,3,8,2,128]{4,2,3,1,0:T(8,128)}, f32[32,3,8,2,128]{4,2,3,1,0:T(8,128)}, u32[]{:S(2)}, u32[]{:S(2)}) collective-permute-start(f32[32,3,8,2,128]{4,2,3,1,0:T(8,128)} %get-tuple-element.11), channel_id=1, source_target_pairs={{0,1},{1,2},{2,3},{4,5},{5,6},{6,7},{8,9},{9,10},{10,11},{12,13},{... | collective-permute-start | bytes 2359304 | tf_op jit(solution)/shard_map/ppermute | solution.py:16
  47.3 9.4 %copy-start.6 = (f32[32,3,2,4,128]{4,2,3,1,0:T(2,128)S(1)}, f32[32,3,2,4,128]{4,2,3,1,0:T(2,128)}, u32[]{:S(2)}) copy-start(f32[32,3,2,4,128]{4,2,3,1,0:T(2,128)} %copy-done.5) | copy-start | bytes 1179652
  47.3 9.4 %copy-start.8 = (f32[32,3,2,4,128]{4,2,3,1,0:T(2,128)S(1)}, f32[32,3,2,4,128]{4,2,3,1,0:T(2,128)}, u32[]{:S(2)}) copy-start(f32[32,3,2,4,128]{4,2,3,1,0:T(2,128)} %copy-done.7) | copy-start | bytes 1179652
  64.7 60.3 %copy-start.4 = (f32[32,6144]{1,0:T(8,128)S(1)}, f32[32,6144]{1,0:T(8,128)}, u32[]{:S(2)}) copy-start(f32[32,6144]{1,0:T(8,128)} %reshape.56) | copy-start | bytes 2359300
  68.3 189.8 %copy-start.9 = (f32[32,6144]{1,0:T(8,128)S(1)}, f32[32,6144]{1,0:T(8,128)}, u32[]{:S(2)}) copy-start(f32[32,6144]{1,0:T(8,128)} %reshape.63) | copy-start | bytes 2359300
Sparse Core Ops, SparseCore 0:
  128.5 126.5 all-reduce.4
where the time goes:
time: 270 us; the launch traced here: 269 us
  waiting for transfers between devices  135 us (50%)
  blocking collectives  42.4 us (16%)
  matrix products  24.7 us (9%)
  local copies, waits for them, and re-layouts  21 us (8%)
  other arithmetic  18.4 us (7%)
  between operations  14.4 us (5%)
  starting transfers between devices  12.9 us (5%)
    psum x1, waiting for transfers between devices, on_device(): lax.psum((product(flat_p, flat_q), product(flat_p, flat_r), product(flat_...  127 us
    psum x1, blocking collectives, on_device(): lax.psum((product(flat_p, flat_q), product(flat_p, flat_r), product(flat_...  42.4 us
    ppermute x2, starting transfers between devices, with_halo(): before = lax.ppermute(last, axis, up)  10.3 us
    ppermute x2, waiting for transfers between devices, with_halo(): before = lax.ppermute(last, axis, up)  8.37 us
    dot_general x6, matrix products, product(): return jnp.dot(left, right.T, precision=exact_mode)  7.32 us
    concatenate x2, other arithmetic, with_halo(): array = jnp.concatenate([before, array, after], axis=dim)  6.55 us
  transfers between devices with their start and end apart: 5, of which 3 were waited for; matrix products, arithmetic and copies ran while one was open for 6% of the time, Pallas kernels for 0%

commit v1 on v0

--- a/solution.py
+++ b/solution.py
@@ -71,15 +71,18 @@
     rhs_r = product(basis_flat, flat_r)
     rhs_q = product(basis_flat, flat_q)
     summed = lax.psum(
-        (
-            product(flat_p, flat_q),
-            product(flat_p, flat_r),
-            product(flat_q, lined_r),
-            product(flat_q, lined_q),
-            jnp.dot(coarse_factor.T, rhs_r, precision=exact_mode),
-            jnp.dot(coarse_factor.T, rhs_q, precision=exact_mode),
+        lax.psum(
+            (
+                product(flat_p, flat_q),
+                product(flat_p, flat_r),
+                product(flat_q, lined_r),
+                product(flat_q, lined_q),
+                jnp.dot(coarse_factor.T, rhs_r, precision=exact_mode),
+                jnp.dot(coarse_factor.T, rhs_q, precision=exact_mode),
+            ),
+            "inner",
         ),
-        ("sub", "inner"),
+        "sub",
     )
     gram_pq, proj_pr, image_lined_r, image_lined_q, mid_r, mid_q = summed
     lower = jnp.linalg.cholesky(gram_pq)

time: 270 us -> 254 us (0.941)
  waiting for transfers between devices: 135 us -> 111 us
  blocking collectives: 42.4 us -> 47.6 us
    psum x1, waiting for transfers between devices: 127 us -> 29.4 us  [on_device(): lax.psum((product(flat_p, flat_q), product(flat_p, flat_r), product(flat_...]
    psum x0 -> x1, waiting for transfers between devices: none -> 73.1 us  [on_device(): lax.psum(lax.psum((product(flat_p, flat_q), product(flat_p, flat_r), prod...]
    psum x0 -> x1, blocking collectives: none -> 36.4 us  [on_device(): lax.psum(lax.psum((product(flat_p, flat_q), product(flat_p, flat_r), prod...]
    psum x1, blocking collectives: 42.4 us -> 11.2 us  [on_device(): lax.psum((product(flat_p, flat_q), product(flat_p, flat_r), product(flat_...]
  transfers between devices with their start and end apart: 5 -> 6, of which waited for: 3 -> 4; matrix products, arithmetic and copies ran while one was open for 6% -> 7% of each run, Pallas kernels for 0% -> 0%
where the time goes in v1:
time: 254 us; the launch traced here: 253 us
  waiting for transfers between devices  111 us (44%)
  blocking collectives  47.6 us (19%)
  matrix products  25.3 us (10%)
  local copies, waits for them, and re-layouts  23.3 us (9%)
  other arithmetic  18.4 us (7%)
  between operations  14.4 us (6%)
  starting transfers between devices  13 us (5%)
    psum x1, waiting for transfers between devices, on_device(): lax.psum(lax.psum((product(flat_p, flat_q), product(flat_p, flat_r), prod...  73.1 us
    psum x1, blocking collectives, on_device(): lax.psum(lax.psum((product(flat_p, flat_q), product(flat_p, flat_r), prod...  36.4 us
    psum x1, waiting for transfers between devices, on_device(): lax.psum((product(flat_p, flat_q), product(flat_p, flat_r), product(flat_...  29.4 us
    psum x1, blocking collectives, on_device(): lax.psum((product(flat_p, flat_q), product(flat_p, flat_r), product(flat_...  11.2 us
    ppermute x2, starting transfers between devices, with_halo(): before = lax.ppermute(last, axis, up)  10.3 us
    ppermute x2, waiting for transfers between devices, with_halo(): before = lax.ppermute(last, axis, up)  8.37 us
    dot_general x6, matrix products, product(): return jnp.dot(left, right.T, precision=exact_mode)  7.31 us
    concatenate x2, other arithmetic, with_halo(): array = jnp.concatenate([before, array, after], axis=dim)  6.55 us
  transfers between devices with their start and end apart: 6, of which 4 were waited for; matrix products, arithmetic and copies ran while one was open for 7% of the time, Pallas kernels for 0%

profile of v1, /device:TPU:0, one launch (start us, length us, event | category | flops | bytes accessed | tf_op | source)
XLA Modules:
  0.0 253.3 jit_solution(14171320542443696128)
XLA Ops:
  7.2 1.3 fusion.37
  8.6 1.3 collective-permute-start
  10.7 6.4 %collective-permute-start.1 = (f32[32,3,2,4,128]{4,0,3,2,1:T(8,128)}, f32[32,3,2,4,128]{4,0,3,2,1:T(8,128)}, u32[]{:S(2)}, u32[]{:S(2)}) collective-permute-start(f32[32,3,2,4,128]{4,0,3,2,1:T(8,128)} %copy.83), channel_id=1, source_target_pairs={{0,4},{4,8},{8,12},{12,16},{16,20},{20,24},{24,28},{1,5},{5,9},{9,... | collective-permute-start | bytes 1179656 | tf_op jit(solution)/shard_map/ppermute | solution.py:16
  17.1 1.3 copy.42
  18.5 2.4 reshape.56
  20.8 1.2 reshape.58
  22.9 8.4 %collective-permute-done.1 = f32[32,3,2,4,128]{4,0,3,2,1:T(8,128)} collective-permute-done((f32[32,3,2,4,128]{4,0,3,2,1:T(8,128)}, f32[32,3,2,4,128]{4,0,3,2,1:T(8,128)}, u32[]{:S(2)}, u32[]{:S(2)}) %collective-permute-start.1) | collective-permute-done | bytes 393248 | tf_op jit(solution)/shard_map/ppermute | solution.py:16
  31.3 1.3 copy.47
  33.4 1.3 fusion.36
  34.6 1.3 collective-permute-start.2
  35.9 3.9 %collective-permute-start.3 = (f32[32,3,8,2,128]{4,2,3,1,0:T(8,128)}, f32[32,3,8,2,128]{4,2,3,1,0:T(8,128)}, u32[]{:S(2)}, u32[]{:S(2)}) collective-permute-start(f32[32,3,8,2,128]{4,2,3,1,0:T(8,128)} %get-tuple-element.17), channel_id=1, source_target_pairs={{0,1},{1,2},{2,3},{4,5},{5,6},{6,7},{8,9},{9,10},{10,11},{12,13},{... | collective-permute-start | bytes 2359304 | tf_op jit(solution)/shard_map/ppermute | solution.py:16
  39.8 1.7 fusion.23
  41.5 2.2 reshape.61
  43.7 1.2 reshape.63
  44.9 2.4 reshape.55
  50.6 6.0 %select_maximum_fusion = f32[32,3,8,8,132]{4,2,3,1,0:T(8,128)S(1)} fusion(f32[32,3,8,2,128]{4,2,3,1,0:T(8,128)} %collective-permute-done.2, f32[32,3,8,2,128]{4,2,3,1,0:T(8,128)} %collective-permute-done.3, f32[32,3,2,4,128]{4,2,3,1,0:T(2,128)} %copy-done.6, f32[32,3,4,4,128]{4,2,3,1,0:T(4,128)S(1)} %copy.42, f32[32,3,2,4,128]{4,2,3,1,0:T(2,128)} %copy-done.8), kind=kLoop, calls=%fused_computation.7 | loop fusion | flops 9732096 | bytes 6389760 | tf_op jit(solution)/shard_map/concatenate | solution.py:18
  56.7 5.1 %fusion.9 = f32[32,3,4,4,128]{4,2,3,1,0:T(4,128)S(1)} fusion(f32[32,3,2,4,128]{4,2,3,1,0:T(2,128)S(1)} %copy-done.9, f32[32,3,4,4,128]{4,2,3,1,0:T(4,128)S(1)} %copy.42, f32[32,3,2,4,128]{4,2,3,1,0:T(2,128)S(1)} %copy-done.7, f32[32,3,8,8,132]{4,2,3,1,0:T(8,128)S(1)} %select_maximum_fusion, f32[32,3,8,2,128]{4,2,3,1,0:T(8,128)} %collective-permute-done.3, ...), kind=kLoop, calls=%fused_computation.35 | loop fusion | flops 6094848 | bytes 7086080 | tf_op jit(solution)/shard_map/add | solution.py:42
  66.4 1.9 fusion.39
  68.3 11.2 %all-reduce.3 = (f32[32,32]{1,0:T(8,128)S(1)}, f32[32,32]{0,1:T(8,128)S(1)}, f32[32,32]{1,0:T(8,128)S(1)}, f32[32,32]{1,0:T(8,128)S(1)}) all-reduce(f32[32,32]{1,0:T(8,128)S(1)} %convolution_bitcast_fusion.4, f32[32,32]{0,1:T(8,128)S(1)} %convolution_bitcast_fusion.5, ...), channel_id=1, replica_groups=mesh['sub'=8,'inner'=4] {'inner'}, use_global_device_ids=true, to_apply=%region_4.5 | all-reduce | flops 4096 | bytes 32768 | tf_op jit(solution)/shard_map/psum | solution.py:74
  79.5 36.4 %all-reduce.1 = (f32[32,32]{1,0:T(8,128)S(1)}, f32[32,32]{0,1:T(8,128)S(1)}, f32[32,32]{1,0:T(8,128)S(1)}, f32[32,32]{1,0:T(8,128)S(1)}) all-reduce(f32[32,32]{1,0:T(8,128)S(1)} %get-tuple-element.11, f32[32,32]{0,1:T(8,128)S(1)} %get-tuple-element.12, ...), channel_id=1, replica_groups=mesh['sub'=8,'inner'=4] {'sub'}, use_global_device_ids=true, to_apply=%region_5.6 | all-reduce | flops 4096 | bytes 32768 | tf_op jit(solution)/shard_map/psum | solution.py:73
  116.0 2.9 %cholesky.18 = f32[32,32]{1,0:T(8,128)S(1)} custom-call(f32[32,32]{1,0:T(8,128)S(1)} %fusion.33), custom_call_target="Cholesky" | custom-call | tf_op jit(solution)/shard_map/jit(cholesky)/cholesky | solution.py:88
  120.3 2.4 custom-call.12
  124.0 2.8 %convolution_subtract_fusion.1 = f32[32,6144]{1,0:T(8,128)} fusion(f32[32,6144]{1,0:T(8,128)} %reshape.58, f32[32,32]{1,0:T(8,128)S(1)} %fusion.31, f32[32,6144]{1,0:T(8,128)S(1)} %reshape.59), kind=kOutput, calls=%fused_computation.5 | convolution fusion | flops 75694080 | bytes 2363392 | tf_op jit(solution)/shard_map/dot_general | solution.py:90
  126.8 2.6 %reshape.60 = f32[32,3,4,4,128]{4,3,2,1,0:T(4,128)} reshape(f32[32,6144]{1,0:T(8,128)} %convolution_subtract_fusion.1) | data formatting | bytes 1572864 | tf_op jit(solution)/shard_map/reshape | solution.py:103
  129.4 2.8 %convolution_add_fusion.2 = f32[32,6144]{1,0:T(8,128)} fusion(f32[32,6144]{1,0:T(8,128)} %reshape.55, f32[32,32]{1,0:T(8,128)S(1)} %fusion.31, f32[32,6144]{1,0:T(8,128)S(1)} %copy-done.5), kind=kOutput, calls=%fused_computation.6 | convolution fusion | flops 75694080 | bytes 2363392 | tf_op jit(solution)/shard_map/dot_general | solution.py:100
  132.3 2.5 %reshape.57 = f32[32,3,4,4,128]{4,3,2,1,0:T(4,128)} reshape(f32[32,6144]{1,0:T(8,128)} %convolution_add_fusion.2) | data formatting | bytes 1572864 | tf_op jit(solution)/shard_map/reshape | solution.py:103
  135.0 29.4 %all-reduce.10.cloned.1.call-done = (f32[1024,32]{0,1:T(8,128)}, f32[1024,32]{0,1:T(8,128)}) async-done(((f32[1024,32]{0,1:T(8,128)}, f32[1024,32]{0,1:T(8,128)}), (f32[1024,32]{0,1:T(8,128)}, f32[1024,32]{0,1:T(8,128)})) %all-reduce.10.cloned.1.call-update) | async-done | bytes 262160 | tf_op jit(solution)/shard_map/psum | solution.py:74
  164.5 1.7 convolution_subtract_fusion
  166.2 73.1 %all-reduce.8.cloned.1.call-done = (f32[1024,32]{0,1:T(8,128)}, f32[1024,32]{0,1:T(8,128)}) async-done(((f32[1024,32]{0,1:T(8,128)}, f32[1024,32]{0,1:T(8,128)}), (f32[1024,32]{0,1:T(8,128)}, f32[1024,32]{0,1:T(8,128)})) %all-reduce.8.cloned.1.call-update) | async-done | bytes 262160 | tf_op jit(solution)/shard_map/psum | solution.py:73
  239.3 1.3 convolution_subtract_fusion.2
  242.3 1.9 convolution_add_fusion.1
  245.1 1.4 reshape.64
  (63 shorter events, 15.9 us)
Async XLA Ops:
  7.2 42.5 %copy-start = (f32[32,1024]{1,0:T(8,128)S(1)}, f32[32,1024]{1,0:T(8,128)}, u32[]{:S(2)}) copy-start(f32[32,1024]{1,0:T(8,128)} %param.17) | copy-start | bytes 393220
  7.2 13.6 %copy-start.12 = (f32[4,4,128]{2,1,0:T(4,128)S(1)}, f32[4,4,128]{2,1,0:T(4,128)}, u32[]{:S(2)}) copy-start(f32[4,4,128]{2,1,0:T(4,128)} %param.14) | copy-start | bytes 24580
  7.2 13.6 %copy-start.2 = (f32[32,3,4,4,128]{4,3,2,1,0:T(4,128)S(1)}, f32[32,3,4,4,128]{4,3,2,1,0:T(4,128)}, u32[]{:S(2)}) copy-start(f32[32,3,4,4,128]{4,3,2,1,0:T(4,128)} %param.12) | copy-start | bytes 2359300
  7.2 157.3 %all-reduce.10.cloned.1.call-start = ((), (), s32[]{:S(2)}) async-start(), calls=%async_computation.1 | async-start | bytes 524288 | tf_op jit(solution)/shard_map/psum | solution.py:74
  8.6 14.0 %collective-permute-start = (f32[32,3,2,4,128]{4,0,3,2,1:T(8,128)S(1)}, f32[32,3,2,4,128]{4,0,3,2,1:T(8,128)S(1)}, u32[]{:S(2)}, u32[]{:S(2)}) collective-permute-start(f32[32,3,2,4,128]{4,0,3,2,1:T(8,128)S(1)} %copy.84), channel_id=1, source_target_pairs={{4,0},{8,4},{12,8},{16,12},{20,16},{24,20},{28,24},{5,1},{9,5},{13... | collective-permute-start | bytes 1179656 | tf_op jit(solution)/shard_map/ppermute | solution.py:17
  10.7 29.1 %copy-start.11 = (f32[1,1,128,128]{3,2,1,0:T(8,128)S(1)}, f32[1,1,128,128]{3,2,1,0:T(8,128)}, u32[]{:S(2)}) copy-start(f32[1,1,128,128]{3,2,1,0:T(8,128)} %param.16) | copy-start | bytes 196612
  10.7 20.6 %collective-permute-start.1 = (f32[32,3,2,4,128]{4,0,3,2,1:T(8,128)}, f32[32,3,2,4,128]{4,0,3,2,1:T(8,128)}, u32[]{:S(2)}, u32[]{:S(2)}) collective-permute-start(f32[32,3,2,4,128]{4,0,3,2,1:T(8,128)} %copy.83), channel_id=1, source_target_pairs={{0,4},{4,8},{8,12},{12,16},{16,20},{20,24},{24,28},{1,5},{5,9},{9,... | collective-permute-start | bytes 1179656 | tf_op jit(solution)/shard_map/ppermute | solution.py:16
  20.8 22.8 %copy-start.3 = (f32[32,3,4,4,128]{4,3,2,1,0:T(4,128)S(1)}, f32[32,3,4,4,128]{4,3,2,1,0:T(4,128)}, u32[]{:S(2)}) copy-start(f32[32,3,4,4,128]{4,3,2,1,0:T(4,128)} %param.15) | copy-start | bytes 2359300
  22.9 9.7 %copy-start.6 = (f32[32,3,2,4,128]{4,2,3,1,0:T(2,128)}, f32[32,3,2,4,128]{4,2,3,1,0:T(2,128)S(1)}, u32[]{:S(2)}) copy-start(f32[32,3,2,4,128]{4,2,3,1,0:T(2,128)S(1)} %copy.45) | copy-start | bytes 1179652
  32.6 0.8 copy-start.8
  32.6 14.7 %copy-start.1 = (f32[32,3,4,4,128]{4,3,2,1,0:T(4,128)S(1)}, f32[32,3,4,4,128]{4,3,2,1,0:T(4,128)}, u32[]{:S(2)}) copy-start(f32[32,3,4,4,128]{4,3,2,1,0:T(4,128)} %param.13) | copy-start | bytes 2359300
  34.6 16.0 %collective-permute-start.2 = (f32[32,3,8,2,128]{4,2,3,1,0:T(8,128)}, f32[32,3,8,2,128]{4,2,3,1,0:T(8,128)}, u32[]{:S(2)}, u32[]{:S(2)}) collective-permute-start(f32[32,3,8,2,128]{4,2,3,1,0:T(8,128)} %get-tuple-element.18), channel_id=1, source_target_pairs={{1,0},{2,1},{3,2},{5,4},{6,5},{7,6},{9,8},{10,9},{11,10},{13,12},{... | collective-permute-start | bytes 2359304 | tf_op jit(solution)/shard_map/ppermute | solution.py:17
  35.9 14.7 %collective-permute-start.3 = (f32[32,3,8,2,128]{4,2,3,1,0:T(8,128)}, f32[32,3,8,2,128]{4,2,3,1,0:T(8,128)}, u32[]{:S(2)}, u32[]{:S(2)}) collective-permute-start(f32[32,3,8,2,128]{4,2,3,1,0:T(8,128)} %get-tuple-element.17), channel_id=1, source_target_pairs={{0,1},{1,2},{2,3},{4,5},{5,6},{6,7},{8,9},{9,10},{10,11},{12,13},{... | collective-permute-start | bytes 2359304 | tf_op jit(solution)/shard_map/ppermute | solution.py:16
  47.3 9.4 %copy-start.7 = (f32[32,3,2,4,128]{4,2,3,1,0:T(2,128)S(1)}, f32[32,3,2,4,128]{4,2,3,1,0:T(2,128)}, u32[]{:S(2)}) copy-start(f32[32,3,2,4,128]{4,2,3,1,0:T(2,128)} %copy-done.6) | copy-start | bytes 1179652
  47.3 9.4 %copy-start.9 = (f32[32,3,2,4,128]{4,2,3,1,0:T(2,128)S(1)}, f32[32,3,2,4,128]{4,2,3,1,0:T(2,128)}, u32[]{:S(2)}) copy-start(f32[32,3,2,4,128]{4,2,3,1,0:T(2,128)} %copy-done.8) | copy-start | bytes 1179652
  64.3 65.1 %copy-start.5 = (f32[32,6144]{1,0:T(8,128)S(1)}, f32[32,6144]{1,0:T(8,128)}, u32[]{:S(2)}) copy-start(f32[32,6144]{1,0:T(8,128)} %reshape.56) | copy-start | bytes 2359300
  65.6 98.9 %copy-start.4 = (f32[32,6144]{1,0:T(8,128)S(1)}, f32[32,6144]{1,0:T(8,128)}, u32[]{:S(2)}) copy-start(f32[32,6144]{1,0:T(8,128)} %reshape.61) | copy-start | bytes 2359300
  126.8 115.5 %copy-start.10 = (f32[32,6144]{1,0:T(8,128)S(1)}, f32[32,6144]{1,0:T(8,128)}, u32[]{:S(2)}) copy-start(f32[32,6144]{1,0:T(8,128)} %reshape.63) | copy-start | bytes 2359300
  134.9 104.4 %all-reduce.8.cloned.1.call-start = ((), (), s32[]{:S(2)}) async-start(), calls=%async_computation | async-start | bytes 524288 | tf_op jit(solution)/shard_map/psum | solution.py:73
Sparse Core Ops, SparseCore 0:
  135.0 29.4 all-reduce.9
  167.9 71.2 all-reduce.7
